TPU v7x, 128 devices: a whole 4x4x4 slice. The times are simulated.
128 devices in a mesh: section: 8 (over y_hi, x), seq: 16 (over z, y_lo, core).
Axes of the slice: x: 4, y: 4 (y_hi: 2, y_lo: 2; y = y_hi * 2 + y_lo), z: 4, core: 2. Of those that a mesh axis runs over, the one named last changes fastest.
Arguments:
- tokens: bfloat16 [8, 4096, 4096], P('section', 'seq'), may hold values from -6 to 6
- norm_gain: bfloat16 [8, 4096], P('section'), may hold values from 0.099609375 to 1.8984375
- w_query: bfloat16 [8, 4096, 2048], P('section', 'seq'), may hold values from -0.09375 to 0.09375
- w_key: bfloat16 [8, 4096, 512], P('section', 'seq'), may hold values from -1.903125 to 1.903125
- w_value: bfloat16 [8, 4096, 512], P('section', 'seq'), may hold values from -0.09375 to 0.09375
Outputs:
- received: bfloat16 [8, 4096, 2048], P('section', 'seq')
All inputs are finite; a program needn't handle non-finite values.
Results may differ from a plain program's by a relative error of at most 0.012.
The roundings to bfloat16 on the way count: a program that leaves them out, or rounds other values in their place, can miss the bound.
Values may be sent and summed in bfloat16 or wider, within the bound.
No kernel may reach another device: no remote copies, remote signals or barrier semaphores. Data moves between devices by JAX's collectives and lax.ppermute only.
A program may use at most 192 MiB of HBM per device.

v0:
```python
import jax
import jax.numpy as jnp
from jax import lax
from jax.sharding import PartitionSpec as P

LOCAL_QUERY_HEADS = 16
LOCAL_KEY_HEADS = 4
HEAD_SIZE = 128


def shifted(block, axis, distance):
    devices = range(lax.axis_size(axis))
    route = [((i - distance) % len(devices), i) for i in devices]
    return lax.ppermute(block, axis, route)


def normalize(rows_in, gain_row):
    wide = rows_in.astype(jnp.float32)
    scale = lax.rsqrt(jnp.mean(wide * wide, axis=-1, keepdims=True) + 1e-05)
    return (wide * scale * gain_row.astype(jnp.float32)).astype(jnp.bfloat16)


def rotate(matrix, positions):
    row_count = matrix.shape[0]
    head_count = matrix.shape[1] // HEAD_SIZE
    half_dim = HEAD_SIZE // 2
    shaped = matrix.reshape(row_count, head_count, HEAD_SIZE)
    freqs = jnp.power(
        jnp.float32(500000.0), -(jnp.arange(half_dim).astype(jnp.float32) * 2.0 / HEAD_SIZE)
    )
    angles = positions[:, None] * freqs[None, :]
    cosine = jnp.cos(angles)[:, None, :]
    sine_part = jnp.sin(angles)[:, None, :]
    first_half = shaped[:, :, :half_dim]
    second_half = shaped[:, :, half_dim:]
    turned = jnp.concatenate(
        [
            first_half * cosine - second_half * sine_part,
            second_half * cosine + first_half * sine_part,
        ],
        axis=2,
    )
    return turned.reshape(row_count, head_count * HEAD_SIZE)


def expand(matrix):
    row_count = matrix.shape[0]
    kv_count = matrix.shape[1] // HEAD_SIZE
    query_group_count = LOCAL_QUERY_HEADS // LOCAL_KEY_HEADS
    wide = jnp.broadcast_to(
        matrix.reshape(row_count, kv_count, 1, HEAD_SIZE),
        (row_count, kv_count, query_group_count, HEAD_SIZE),
    )
    return wide.reshape(row_count, kv_count * query_group_count * HEAD_SIZE)


def attend(queries, key_rows, value_rows):
    row_count = queries.shape[0]
    head_count = queries.shape[1] // HEAD_SIZE
    block_rows = min(512, row_count)
    key_heads = key_rows.reshape(row_count, head_count, HEAD_SIZE)
    value_heads = value_rows.reshape(row_count, head_count, HEAD_SIZE)
    key_places = jnp.arange(row_count)

    def one_block(block_index):
        first_row = block_index * block_rows
        query_block = lax.dynamic_slice_in_dim(queries, first_row, block_rows, 0).reshape(
            block_rows, head_count, HEAD_SIZE
        )
        scores = jnp.einsum(
            "qhd,khd->hqk", query_block, key_heads, preferred_element_type=jnp.float32
        ) / jnp.sqrt(jnp.float32(HEAD_SIZE))
        query_places = first_row + jnp.arange(block_rows)
        causal = key_places[None, :] <= query_places[:, None]
        scores = jnp.where(causal[None, :, :], scores, -jnp.inf)
        maxima = jnp.max(scores, axis=-1, keepdims=True)
        expon = jnp.exp(scores - maxima)
        probs = (expon / jnp.sum(expon, axis=-1, keepdims=True)).astype(jnp.bfloat16)
        mixed = jnp.einsum("hqk,khd->qhd", probs, value_heads, preferred_element_type=jnp.float32)
        return mixed.astype(jnp.bfloat16).reshape(block_rows, head_count * HEAD_SIZE)

    blocks = lax.map(one_block, jnp.arange(row_count // block_rows))
    return blocks.reshape(row_count, head_count * HEAD_SIZE)


def per_device(tokens, norm_gain, w_query, w_key, w_value):
    normed = normalize(tokens[0], norm_gain[0])
    local_rows = normed.shape[0]
    query_weight = w_query[0]
    key_weight = w_key[0]
    value_weight = w_value[0]
    pieces = (
        lax.all_gather(query_weight, "seq", axis=0, tiled=True),
        lax.all_gather(key_weight, "seq", axis=0, tiled=True),
        lax.all_gather(value_weight, "seq", axis=0, tiled=True),
    )
    query_raw, key_raw, value_raw = tuple(
        (jnp.dot(normed, piece, preferred_element_type=jnp.float32) for piece in pieces)
    )
    positions = (lax.axis_index("seq") * local_rows + jnp.arange(local_rows)).astype(jnp.float32)
    queries = rotate(query_raw, positions).astype(jnp.bfloat16)
    key_rows = expand(rotate(key_raw, positions).astype(jnp.bfloat16))
    value_rows = expand(value_raw.astype(jnp.bfloat16))
    head_queries, head_keys, head_values = (
        lax.all_to_all(queries, "seq", split_axis=1, concat_axis=0, tiled=True),
        lax.all_to_all(key_rows, "seq", split_axis=1, concat_axis=0, tiled=True),
        lax.all_to_all(value_rows, "seq", split_axis=1, concat_axis=0, tiled=True),
    )
    attended = attend(head_queries, head_keys, head_values)
    token_layout = lax.all_to_all(attended, "seq", split_axis=0, concat_axis=1, tiled=True)
    arrived = shifted(token_layout, "section", 1)
    return arrived[None]


def solution(mesh):
    return jax.shard_map(
        per_device,
        mesh=mesh,
        in_specs=(
            P("section", "seq", None),
            P("section", None),
            P("section", "seq", None),
            P("section", "seq", None),
            P("section", "seq", None),
        ),
        out_specs=P("section", "seq", None),
        check_vma=False,
    )
```

profile of v0, /device:TPU:0, one launch (start us, length us, event | category | flops | bytes accessed | tf_op | source)
XLA Modules:
  0.0 348.0 jit_solution(4514223311323205779)
XLA Ops:
  11.9 37.0 %all-gather.9.cloned.1.call-done = bf16[1,4096,512]{2,1,0:T(8,128)(2,1)} async-done(((bf16[1,256,512]{2,1,0:T(8,128)(2,1)}), bf16[1,4096,512]{2,1,0:T(8,128)(2,1)}) %all-gather.9.cloned.1.call-update) | async-done | bytes 4194320 | tf_op jit(solution)/shard_map/all_gather | solution.py:94
  48.9 6.5 %copy.24 = bf16[512,4096]{1,0:T(8,128)(2,1)} copy(bf16[512,4096]{0,1:T(8,128)(2,1)} %bitcast.89) | data formatting | bytes 8388608 | tf_op jit(solution)/shard_map/dot_general | solution.py:98
  55.4 3.5 %fusion.34 = f32[256,4,128]{0,2,1:T(8,128)S(1)} fusion(bf16[4,128,4096]{2,1,0:T(8,128)(2,1)} %bitcast.90, bf16[1,256,4096]{2,1,0:T(8,128)(2,1)S(1)} %copy-done, f32[4096]{0:T(1024)S(1)} %bitcast.99, f32[256]{0:T(256)S(1)} %add_rsqrt_fusion), kind=kOutput, calls=%fused_computation.34 | convolution fusion | flops 1077936128 | bytes 6833152 | tf_op jit(solution)/shard_map/dot_general | solution.py:98
  60.5 4.2 %all-to-all-start.1 = ((bf16[256,16,128]{2,0,1:T(8,128)(2,1)}), bf16[256,16,128]{2,0,1:T(8,128)(2,1)S(1)}, u32[]{:S(2)}, u32[]{:S(2)}) async-start(bf16[256,16,128]{2,0,1:T(8,128)(2,1)} %bitcast.12), calls=%async_computation.1 | async-start | bytes 2097152 | tf_op jit(solution)/shard_map/all_to_all | solution.py:106
  64.6 88.7 %all-gather.7.cloned.1.call-done = bf16[1,4096,2048]{2,1,0:T(8,128)(2,1)} async-done(((bf16[1,256,2048]{2,1,0:T(8,128)(2,1)}), bf16[1,4096,2048]{2,1,0:T(8,128)(2,1)}) %all-gather.7.cloned.1.call-update) | async-done | bytes 16777232 | tf_op jit(solution)/shard_map/all_gather | solution.py:93
  153.4 20.7 %copy.22 = bf16[2048,4096]{1,0:T(8,128)(2,1)} copy(bf16[2048,4096]{0,1:T(8,128)(2,1)} %bitcast.87) | data formatting | bytes 33554432 | tf_op jit(solution)/shard_map/dot_general | solution.py:98
  174.1 8.5 %fusion.36 = f32[256,16,128]{0,2,1:T(8,128)S(1)} fusion(bf16[16,128,4096]{2,1,0:T(8,128)(2,1)} %bitcast.88, bf16[1,256,4096]{2,1,0:T(8,128)(2,1)S(1)} %copy-done, f32[4096]{0:T(1024)S(1)} %bitcast.100, f32[256]{0:T(256)S(1)} %add_rsqrt_fusion), kind=kOutput, calls=%fused_computation.35 | convolution fusion | flops 4299161600 | bytes 20988928 | tf_op jit(solution)/shard_map/dot_general | solution.py:98
  185.0 4.9 %all-to-all-start = ((bf16[256,16,128]{0,2,1:T(8,128)(2,1)}), bf16[256,16,128]{0,2,1:T(8,128)(2,1)S(1)}, u32[]{:S(2)}, u32[]{:S(2)}) async-start(bf16[256,16,128]{0,2,1:T(8,128)(2,1)} %pad_maximum_fusion), calls=%async_computation | async-start | bytes 2097152 | tf_op jit(solution)/shard_map/all_to_all | solution.py:105
  189.9 3.6 %all-gather.11.cloned.1.call-done = bf16[1,4096,512]{2,1,0:T(8,128)(2,1)} async-done(((bf16[1,256,512]{2,1,0:T(8,128)(2,1)}), bf16[1,4096,512]{2,1,0:T(8,128)(2,1)}) %all-gather.11.cloned.1.call-update) | async-done | bytes 4194320 | tf_op jit(solution)/shard_map/all_gather | solution.py:95
  193.5 3.5 fusion.29
  197.0 9.4 %all-to-all-done = bf16[256,16,128]{0,2,1:T(8,128)(2,1)S(1)} async-done(((bf16[256,16,128]{0,2,1:T(8,128)(2,1)}), bf16[256,16,128]{0,2,1:T(8,128)(2,1)S(1)}, u32[]{:S(2)}, u32[]{:S(2)}) %all-to-all-start) | async-done | bytes 1048608 | tf_op jit(solution)/shard_map/all_to_all | solution.py:105
  207.6 3.8 %all-to-all-start.2 = ((bf16[256,16,128]{2,0,1:T(8,128)(2,1)}), bf16[256,16,128]{2,0,1:T(8,128)(2,1)S(1)}, u32[]{:S(2)}, u32[]{:S(2)}) async-start(bf16[256,16,128]{2,0,1:T(8,128)(2,1)} %bitcast.16), calls=%async_computation.2 | async-start | bytes 2097152 | tf_op jit(solution)/shard_map/all_to_all | solution.py:107
  212.8 15.0 %all-to-all-done.2 = bf16[256,16,128]{2,0,1:T(8,128)(2,1)S(1)} async-done(((bf16[256,16,128]{2,0,1:T(8,128)(2,1)}), bf16[256,16,128]{2,0,1:T(8,128)(2,1)S(1)}, u32[]{:S(2)}, u32[]{:S(2)}) %all-to-all-start.2) | async-done | bytes 1048608 | tf_op jit(solution)/shard_map/all_to_all | solution.py:107
  227.8 63.7 %while.11 = (s32[]{:T(128)}, bf16[8,512,128]{2,1,0:T(8,128)(2,1)}, s32[8]{0:T(128)S(1)}, bf16[4096,128]{1,0:T(8,128)(2,1)}, bf16[4096,1,128]{2,0,1:T(8,128)(2,1)...) while((s32[]{:T(128)}, bf16[8,512,128]{2,1,0:T(8,128)(2,1)}, ...), condition=%wide.region_4.5_spmd.clone, body=%wide.region_1.4_spmd.clone.sunk | while | flops 1092681216 | bytes 27539636 | solution.py:82
  232.9 2.8 fusion.48
  240.9 2.8 fusion.48
  248.8 2.8 fusion.48
  256.8 2.8 fusion.48
  264.8 2.8 fusion.48
  272.7 2.8 fusion.48
  280.7 2.8 fusion.48
  288.7 2.8 fusion.48
  291.5 20.1 %all_to_all.67 = bf16[16,256,128]{2,1,0:T(8,128)(2,1)S(1)} all-to-all(bf16[16,256,128]{2,1,0:T(8,128)(2,1)} %bitcast.96), channel_id=1, replica_groups=mesh['section'=8,'seq'=16] {'seq'}, dimensions={0} | all-to-all | bytes 2097152 | tf_op jit(solution)/shard_map/all_to_all | solution.py:110
  313.6 26.4 %collective-permute-done = bf16[256,2048]{0,1:T(8,128)(2,1)S(1)} collective-permute-done((bf16[256,2048]{0,1:T(8,128)(2,1)S(1)}, bf16[256,2048]{0,1:T(8,128)(2,1)S(1)}, u32[]{:S(2)}, u32[]{:S(2)}) %collective-permute-start) | collective-permute-done | bytes 1048608 | tf_op jit(solution)/shard_map/ppermute | solution.py:14
  (65 shorter events, 51.1 us)
Async XLA Ops:
  6.5 42.4 %all-gather.9.cloned.1.call-start = ((), (), s32[]{:S(2)}) async-start(), calls=%async_computation.5 | async-start | bytes 4456448 | tf_op jit(solution)/shard_map/all_gather | solution.py:94
  7.3 146.1 %all-gather.7.cloned.1.call-start = ((), (), s32[]{:S(2)}) async-start(), calls=%async_computation.4 | async-start | bytes 17825792 | tf_op jit(solution)/shard_map/all_gather | solution.py:93
  8.0 185.5 %all-gather.11.cloned.1.call-start = ((), (), s32[]{:S(2)}) async-start(), calls=%async_computation.6 | async-start | bytes 4456448 | tf_op jit(solution)/shard_map/all_gather | solution.py:95
  48.9 6.5 %copy-start = (bf16[1,256,4096]{2,1,0:T(8,128)(2,1)S(1)}, bf16[1,256,4096]{2,1,0:T(8,128)(2,1)}, u32[]{:S(2)}) copy-start(bf16[1,256,4096]{2,1,0:T(8,128)(2,1)} %param.7) | copy-start | bytes 6291460
  60.5 123.5 %all-to-all-start.1 = ((bf16[256,16,128]{2,0,1:T(8,128)(2,1)}), bf16[256,16,128]{2,0,1:T(8,128)(2,1)S(1)}, u32[]{:S(2)}, u32[]{:S(2)}) async-start(bf16[256,16,128]{2,0,1:T(8,128)(2,1)} %bitcast.12), calls=%async_computation.1 | async-start | bytes 2097152 | tf_op jit(solution)/shard_map/all_to_all | solution.py:106
  184.0 1.0 copy-start.1
  185.0 21.5 %all-to-all-start = ((bf16[256,16,128]{0,2,1:T(8,128)(2,1)}), bf16[256,16,128]{0,2,1:T(8,128)(2,1)S(1)}, u32[]{:S(2)}, u32[]{:S(2)}) async-start(bf16[256,16,128]{0,2,1:T(8,128)(2,1)} %pad_maximum_fusion), calls=%async_computation | async-start | bytes 2097152 | tf_op jit(solution)/shard_map/all_to_all | solution.py:105
  196.9 30.8 %copy-start.2 = (bf16[256,16,128]{2,0,1:T(8,128)(2,1)S(1)}, bf16[256,16,128]{2,0,1:T(8,128)(2,1)}, u32[]{:S(2)}) copy-start(bf16[256,16,128]{2,0,1:T(8,128)(2,1)} %copy-done.1) | copy-start | bytes 3145732
  207.6 20.2 %all-to-all-start.2 = ((bf16[256,16,128]{2,0,1:T(8,128)(2,1)}), bf16[256,16,128]{2,0,1:T(8,128)(2,1)S(1)}, u32[]{:S(2)}, u32[]{:S(2)}) async-start(bf16[256,16,128]{2,0,1:T(8,128)(2,1)} %bitcast.16), calls=%async_computation.2 | async-start | bytes 2097152 | tf_op jit(solution)/shard_map/all_to_all | solution.py:107
  312.1 28.0 %collective-permute-start = (bf16[256,2048]{0,1:T(8,128)(2,1)S(1)}, bf16[256,2048]{0,1:T(8,128)(2,1)S(1)}, u32[]{:S(2)}, u32[]{:S(2)}) collective-permute-start(bf16[256,2048]{0,1:T(8,128)(2,1)S(1)} %bitcast.97), channel_id=1, source_target_pairs={{112,0},{0,16},{16,32},{32,48},{48,64},{64,80},{80,96},{96,112},{1... | collective-permute-start | bytes 3145736 | tf_op jit(solution)/shard_map/ppermute | solution.py:14
Sparse Core Ops, SparseCore 0:
  9.0 39.8 all-gather.8
  50.6 102.7 all-gather.6
  155.1 38.3 all-gather.10
where the time goes:
time: 349 us; the launch traced here: 348 us
  waiting for transfers between devices  182 us (52%)
  matrix products  58.8 us (17%)
  local copies, waits for them, and re-layouts  39 us (11%)
  blocking collectives  20.1 us (6%)
  other arithmetic  14.9 us (4%)
  starting transfers between devices  14.5 us (4%)
  between operations  13.2 us (4%)
  loops' own time  5.19 us (1%)
    all_gather x1, waiting for transfers between devices, per_device(): lax.all_gather(query_weight, 'seq', axis=0, tiled=True)  88.7 us
    all_gather x1, waiting for transfers between devices, per_device(): lax.all_gather(key_weight, 'seq', axis=0, tiled=True)  37 us
    dot_general x2, local copies, waits for them, and re-layouts, per_device(): jnp.dot(normed, piece, preferred_element_type=jnp.float32)  27.3 us
    ppermute x1, waiting for transfers between devices, shifted(): return lax.ppermute(block, axis, route)  26.4 us
    dot_general x8, matrix products, one_block(): jnp.einsum('hqk,khd->qhd', probs, value_heads, preferred_element_type=jnp...  22.6 us
    dot_general x8, matrix products, one_block(): jnp.einsum('qhd,khd->hqk', query_block, key_heads, preferred_element_type...  20.7 us
    all_to_all x1, blocking collectives, per_device(): lax.all_to_all(attended, 'seq', split_axis=0, concat_axis=1, tiled=True)  20.1 us
    dot_general x3, matrix products, per_device(): jnp.dot(normed, piece, preferred_element_type=jnp.float32)  15.5 us
  transfers between devices with their start and end apart: 7, of which 6 were waited for; matrix products, arithmetic and copies ran while one was open for 14% of the time, Pallas kernels for 0%

commit v1 on v0

--- a/solution.py
+++ b/solution.py
@@ -90,7 +90,9 @@
     key_weight = w_key[0]
     value_weight = w_value[0]
     pieces = (
-        lax.all_gather(query_weight, "seq", axis=0, tiled=True),
+        jnp.concatenate(
+            lax.all_to_all(jnp.stack([query_weight] * lax.axis_size("seq")), "seq", 0, 0), axis=0
+        ),
         lax.all_gather(key_weight, "seq", axis=0, tiled=True),
         lax.all_gather(value_weight, "seq", axis=0, tiled=True),
     )

time: 349 us -> 476 us (1.36)
  waiting for transfers between devices: 182 us -> 271 us
  local copies, waits for them, and re-layouts: 39 us -> 68.3 us
  starting transfers between devices: 14.5 us -> 25.3 us
    all_gather x1, waiting for transfers between devices: 37 us -> 209 us  [per_device(): lax.all_gather(key_weight, 'seq', axis=0, tiled=True)]
    all_gather x1 -> x0, waiting for transfers between devices: 88.7 us -> none  [per_device(): lax.all_gather(query_weight, 'seq', axis=0, tiled=True)]
    all_to_all x0 -> x1, local copies, waits for them, and re-layouts: none -> 21.8 us  [per_device(): lax.all_to_all(jnp.stack([query_weight] * lax.axis_size('seq')), 'seq', 0...]
    another operation x0 -> x2, local copies, waits for them, and re-layouts: none -> 7.39 us  [the longest x1 5.91 us: per_device(): jnp.stack([query_weight] * lax.axis_size('seq'))]
    all_to_all x0 -> x1, starting transfers between devices: none -> 6.72 us  [per_device(): lax.all_to_all(jnp.stack([query_weight] * lax.axis_size('seq')), 'seq', 0...]
    all_to_all x0 -> x1, waiting for transfers between devices: none -> 6.04 us  [per_device(): lax.all_to_all(jnp.stack([query_weight] * lax.axis_size('seq')), 'seq', 0...]
  transfers between devices with their start and end apart: 7 -> 7, of which waited for: 6 -> 5; matrix products, arithmetic and copies ran while one was open for 14% -> 15% of each run, Pallas kernels for 0% -> 0%
where the time goes in v1:
time: 476 us; the launch traced here: 474 us
  waiting for transfers between devices  271 us (57%)
  local copies, waits for them, and re-layouts  68.3 us (14%)
  matrix products  58.6 us (12%)
  starting transfers between devices  25.3 us (5%)
  blocking collectives  20.1 us (4%)
  between operations  13.6 us (3%)
  other arithmetic  12.6 us (3%)
  loops' own time  5.19 us (1%)
    all_gather x1, waiting for transfers between devices, per_device(): lax.all_gather(key_weight, 'seq', axis=0, tiled=True)  209 us
    dot_general x2, local copies, waits for them, and re-layouts, per_device(): jnp.dot(normed, piece, preferred_element_type=jnp.float32)  27.3 us
    ppermute x1, waiting for transfers between devices, shifted(): return lax.ppermute(block, axis, route)  26.4 us
    dot_general x8, matrix products, one_block(): jnp.einsum('hqk,khd->qhd', probs, value_heads, preferred_element_type=jnp...  22.6 us
    all_to_all x1, local copies, waits for them, and re-layouts, per_device(): lax.all_to_all(jnp.stack([query_weight] * lax.axis_size('seq')), 'seq', 0...  21.8 us
    dot_general x8, matrix products, one_block(): jnp.einsum('qhd,khd->hqk', query_block, key_heads, preferred_element_type...  20.7 us
    all_to_all x1, blocking collectives, per_device(): lax.all_to_all(attended, 'seq', split_axis=0, concat_axis=1, tiled=True)  20.1 us
    dot_general x3, matrix products, per_device(): jnp.dot(normed, piece, preferred_element_type=jnp.float32)  15.3 us
  transfers between devices with their start and end apart: 7, of which 5 were waited for; matrix products, arithmetic and copies ran while one was open for 15% of the time, Pallas kernels for 0%

profile of v1, /device:TPU:0, one launch (start us, length us, event | category | flops | bytes accessed | tf_op | source)
XLA Modules:
  0.0 474.2 jit_solution(3716623746996823905)
XLA Ops:
  8.0 5.9 %stack.3 = bf16[16,256,2048]{1,2,0:T(8,128)(2,1)} broadcast(bf16[256,2048]{0,1:T(8,128)(2,1)S(1)} %copy.22), dimensions={1,2} | broadcast | bytes 17825792 | tf_op jit(solution)/shard_map/stack | solution.py:94
  13.9 6.7 %all-to-all-start = ((bf16[16,256,2048]{1,2,0:T(8,128)(2,1)}), bf16[16,256,2048]{1,2,0:T(8,128)(2,1)}, u32[]{:S(2)}, u32[]{:S(2)}) async-start(bf16[16,256,2048]{1,2,0:T(8,128)(2,1)} %stack.3), calls=%async_computation | async-start | bytes 33554432 | tf_op jit(solution)/shard_map/all_to_all | solution.py:94
  23.1 208.7 %all-gather.5.cloned.1.call-done = bf16[1,4096,512]{2,1,0:T(8,128)(2,1)} async-done(((bf16[1,256,512]{2,1,0:T(8,128)(2,1)}), bf16[1,4096,512]{2,1,0:T(8,128)(2,1)}) %all-gather.5.cloned.1.call-update) | async-done | bytes 4194320 | tf_op jit(solution)/shard_map/all_gather | solution.py:96
  231.8 6.4 %copy.26 = bf16[512,4096]{1,0:T(8,128)(2,1)} copy(bf16[512,4096]{0,1:T(8,128)(2,1)} %bitcast.90) | data formatting | bytes 8388608 | tf_op jit(solution)/shard_map/dot_general | solution.py:100
  238.2 3.5 fusion.34
  242.0 6.0 %all-to-all-done = bf16[16,256,2048]{1,2,0:T(8,128)(2,1)} async-done(((bf16[16,256,2048]{1,2,0:T(8,128)(2,1)}), bf16[16,256,2048]{1,2,0:T(8,128)(2,1)}, u32[]{:S(2)}, u32[]{:S(2)}) %all-to-all-start) | async-done | bytes 16777248 | tf_op jit(solution)/shard_map/all_to_all | solution.py:94
  249.3 7.4 %all-to-all-start.2 = ((bf16[256,16,128]{2,0,1:T(8,128)(2,1)}), bf16[256,16,128]{2,0,1:T(8,128)(2,1)S(1)}, u32[]{:S(2)}, u32[]{:S(2)}) async-start(bf16[256,16,128]{2,0,1:T(8,128)(2,1)} %bitcast.13), calls=%async_computation.2 | async-start | bytes 2097152 | tf_op jit(solution)/shard_map/all_to_all | solution.py:108
  256.7 21.8 %copy.23 = bf16[16,256,2048]{2,1,0:T(8,128)(2,1)} copy(bf16[16,256,2048]{1,2,0:T(8,128)(2,1)} %all-to-all-done) | data formatting | bytes 33554432 | tf_op jit(solution)/shard_map/all_to_all | solution.py:94
  278.5 20.9 %copy.24 = bf16[2048,4096]{1,0:T(8,128)(2,1)} copy(bf16[2048,4096]{0,1:T(8,128)(2,1)} %bitcast.88) | data formatting | bytes 33554432 | tf_op jit(solution)/shard_map/dot_general | solution.py:100
  299.4 8.3 %fusion.36 = f32[256,16,128]{0,2,1:T(8,128)S(1)} fusion(bf16[16,128,4096]{2,1,0:T(8,128)(2,1)} %bitcast.89, bf16[1,256,4096]{2,1,0:T(8,128)(2,1)S(1)} %copy-done, f32[4096]{0:T(1024)S(1)} %bitcast.102, f32[256]{0:T(256)S(1)} %add_rsqrt_fusion), kind=kOutput, calls=%fused_computation.35 | convolution fusion | flops 4299161600 | bytes 20988928 | tf_op jit(solution)/shard_map/dot_general | solution.py:100
  310.1 5.7 %all-to-all-start.1 = ((bf16[256,16,128]{0,2,1:T(8,128)(2,1)}), bf16[256,16,128]{0,2,1:T(8,128)(2,1)S(1)}, u32[]{:S(2)}, u32[]{:S(2)}) async-start(bf16[256,16,128]{0,2,1:T(8,128)(2,1)} %pad_maximum_fusion), calls=%async_computation.1 | async-start | bytes 2097152 | tf_op jit(solution)/shard_map/all_to_all | solution.py:107
  315.8 3.5 fusion.29
  319.3 13.0 %all-to-all-done.1 = bf16[256,16,128]{0,2,1:T(8,128)(2,1)S(1)} async-done(((bf16[256,16,128]{0,2,1:T(8,128)(2,1)}), bf16[256,16,128]{0,2,1:T(8,128)(2,1)S(1)}, u32[]{:S(2)}, u32[]{:S(2)}) %all-to-all-start.1) | async-done | bytes 1048608 | tf_op jit(solution)/shard_map/all_to_all | solution.py:107
  333.5 3.8 all-to-all-start.3
  338.6 15.0 %all-to-all-done.3 = bf16[256,16,128]{2,0,1:T(8,128)(2,1)S(1)} async-done(((bf16[256,16,128]{2,0,1:T(8,128)(2,1)}), bf16[256,16,128]{2,0,1:T(8,128)(2,1)S(1)}, u32[]{:S(2)}, u32[]{:S(2)}) %all-to-all-start.3) | async-done | bytes 1048608 | tf_op jit(solution)/shard_map/all_to_all | solution.py:109
  353.6 63.7 %while.11 = (s32[]{:T(128)}, bf16[8,512,128]{2,1,0:T(8,128)(2,1)}, s32[8]{0:T(128)S(1)}, bf16[4096,128]{1,0:T(8,128)(2,1)}, bf16[4096,1,128]{2,0,1:T(8,128)(2,1)...) while((s32[]{:T(128)}, bf16[8,512,128]{2,1,0:T(8,128)(2,1)}, ...), condition=%wide.region_4.5_spmd.clone, body=%wide.region_1.4_spmd.clone.sunk | while | flops 1092681216 | bytes 27540136 | solution.py:82
  358.8 2.8 fusion.48
  366.7 2.8 fusion.48
  374.7 2.8 fusion.48
  382.7 2.8 fusion.48
  398.6 2.8 fusion.48
  414.5 2.8 fusion.48
  417.4 20.1 %all_to_all.72 = bf16[16,256,128]{2,1,0:T(8,128)(2,1)S(1)} all-to-all(bf16[16,256,128]{2,1,0:T(8,128)(2,1)} %bitcast.98), channel_id=1, replica_groups=mesh['section'=8,'seq'=16] {'seq'}, dimensions={0} | all-to-all | bytes 2097152 | tf_op jit(solution)/shard_map/all_to_all | solution.py:112
  439.5 26.4 %collective-permute-done = bf16[256,2048]{0,1:T(8,128)(2,1)S(1)} collective-permute-done((bf16[256,2048]{0,1:T(8,128)(2,1)S(1)}, bf16[256,2048]{0,1:T(8,128)(2,1)S(1)}, u32[]{:S(2)}, u32[]{:S(2)}) %collective-permute-start) | collective-permute-done | bytes 1048608 | tf_op jit(solution)/shard_map/ppermute | solution.py:14
  (69 shorter events, 55.3 us)
Async XLA Ops:
  13.9 8.2 %copy-start.3 = (bf16[1,4096]{1,0:T(2,128)(2,1)S(1)}, bf16[1,4096]{1,0:T(2,128)(2,1)}, u32[]{:S(2)}) copy-start(bf16[1,4096]{1,0:T(2,128)(2,1)} %param.8) | copy-start | bytes 24580
  13.9 8.3 %copy-start = (bf16[1,256,4096]{2,1,0:T(8,128)(2,1)S(1)}, bf16[1,256,4096]{2,1,0:T(8,128)(2,1)}, u32[]{:S(2)}) copy-start(bf16[1,256,4096]{2,1,0:T(8,128)(2,1)} %param.7) | copy-start | bytes 6291460
  13.9 234.1 %all-to-all-start = ((bf16[16,256,2048]{1,2,0:T(8,128)(2,1)}), bf16[16,256,2048]{1,2,0:T(8,128)(2,1)}, u32[]{:S(2)}, u32[]{:S(2)}) async-start(bf16[16,256,2048]{1,2,0:T(8,128)(2,1)} %stack.3), calls=%async_computation | async-start | bytes 33554432 | tf_op jit(solution)/shard_map/all_to_all | solution.py:94
  20.7 211.1 %all-gather.5.cloned.1.call-start = ((), (), s32[]{:S(2)}) async-start(), calls=%async_computation.5 | async-start | bytes 4456448 | tf_op jit(solution)/shard_map/all_gather | solution.py:96
  21.4 294.4 %all-gather.7.cloned.1.call-start = ((), (), s32[]{:S(2)}) async-start(), calls=%async_computation.6 | async-start | bytes 4456448 | tf_op jit(solution)/shard_map/all_gather | solution.py:97
  249.3 59.8 %all-to-all-start.2 = ((bf16[256,16,128]{2,0,1:T(8,128)(2,1)}), bf16[256,16,128]{2,0,1:T(8,128)(2,1)S(1)}, u32[]{:S(2)}, u32[]{:S(2)}) async-start(bf16[256,16,128]{2,0,1:T(8,128)(2,1)} %bitcast.13), calls=%async_computation.2 | async-start | bytes 2097152 | tf_op jit(solution)/shard_map/all_to_all | solution.py:108
  309.1 1.0 copy-start.1
  310.1 22.2 %all-to-all-start.1 = ((bf16[256,16,128]{0,2,1:T(8,128)(2,1)}), bf16[256,16,128]{0,2,1:T(8,128)(2,1)S(1)}, u32[]{:S(2)}, u32[]{:S(2)}) async-start(bf16[256,16,128]{0,2,1:T(8,128)(2,1)} %pad_maximum_fusion), calls=%async_computation.1 | async-start | bytes 2097152 | tf_op jit(solution)/shard_map/all_to_all | solution.py:107
  319.3 34.4 %copy-start.2 = (bf16[256,16,128]{2,0,1:T(8,128)(2,1)S(1)}, bf16[256,16,128]{2,0,1:T(8,128)(2,1)}, u32[]{:S(2)}) copy-start(bf16[256,16,128]{2,0,1:T(8,128)(2,1)} %copy-done.1) | copy-start | bytes 3145732
  333.5 20.2 %all-to-all-start.3 = ((bf16[256,16,128]{2,0,1:T(8,128)(2,1)}), bf16[256,16,128]{2,0,1:T(8,128)(2,1)S(1)}, u32[]{:S(2)}, u32[]{:S(2)}) async-start(bf16[256,16,128]{2,0,1:T(8,128)(2,1)} %bitcast.17), calls=%async_computation.3 | async-start | bytes 2097152 | tf_op jit(solution)/shard_map/all_to_all | solution.py:109
  437.9 28.0 %collective-permute-start = (bf16[256,2048]{0,1:T(8,128)(2,1)S(1)}, bf16[256,2048]{0,1:T(8,128)(2,1)S(1)}, u32[]{:S(2)}, u32[]{:S(2)}) collective-permute-start(bf16[256,2048]{0,1:T(8,128)(2,1)S(1)} %bitcast.99), channel_id=1, source_target_pairs={{112,0},{0,16},{16,32},{32,48},{48,64},{64,80},{80,96},{96,112},{1... | collective-permute-start | bytes 3145736 | tf_op jit(solution)/shard_map/ppermute | solution.py:14
Sparse Core Ops, SparseCore 0:
  23.2 208.5 all-gather.4
  233.5 56.7 all-gather.6
